TPU v7x, 32 devices: a whole 2x2x4 slice. The times are simulated.
32 devices in a mesh: fsdp: 8 (over y, x, core), dp: 4 (over z).
Axes of the slice: x: 2, y: 2, z: 4, core: 2. Of those that a mesh axis runs over, the one named last changes fastest.
Arguments:
- tokens: bfloat16 [16384, 4096], P(('fsdp', 'dp')), may hold values from -40 to 40
- cotangent: bfloat16 [16384, 2048], P(('fsdp', 'dp')), may hold values from -20 to 20
- weight: bfloat16 [4096, 2048], P('fsdp'), may hold values from -1 to 1
- left_vector: float32 [4096], P('fsdp'), may hold values from -6 to 6
Outputs:
- layer_out: bfloat16 [16384, 2048], P(('fsdp', 'dp'))
- input_grad: bfloat16 [16384, 4096], P(('fsdp', 'dp'))
- update: bfloat16 [4096, 2048], P('fsdp')
- left_next: float32 [4096], P('fsdp')
- right_next: float32 [2048], replicated
All inputs are finite; a program needn't handle non-finite values.
Results may differ from a plain program's by a relative error of at most 0.015.
Values may be sent and summed in bfloat16 or wider, within the bound.
A program may use at most 128 MiB of HBM per device.

v0:
```python
import jax
import jax.numpy as jnp
from jax import lax
from jax.sharding import PartitionSpec as P

epsilon = 1e-06


def per_device(tokens, cotangent, weight, left_vector):
    highest = lax.Precision.HIGHEST
    weight_wide = weight.astype(jnp.float32)
    part_right = jnp.dot(left_vector, weight_wide, precision=highest)
    right_raw = lax.psum(part_right, "fsdp")
    right_next = right_raw / jnp.sqrt(jnp.sum(right_raw * right_raw) + epsilon)
    left_raw = jnp.dot(weight_wide, right_next, precision=highest)
    left_sq = lax.psum(jnp.sum(left_raw * left_raw), "fsdp")
    spectral = jnp.sqrt(left_sq + epsilon)
    left_next = left_raw / spectral
    gathered = lax.all_gather(weight, "fsdp", axis=0, tiled=True)
    product = jnp.dot(tokens, gathered, preferred_element_type=jnp.float32)
    layer_out = (product / spectral).astype(jnp.bfloat16)
    back_prod = lax.dot_general(
        cotangent, gathered, (((1,), (1,)), ((), ())), preferred_element_type=jnp.float32
    )
    input_grad = (back_prod / spectral).astype(jnp.bfloat16)
    shard_rows = weight.shape[0]
    shard_sum = lax.psum_scatter(
        lax.dot_general(
            tokens, cotangent, (((0,), (0,)), ((), ())), preferred_element_type=jnp.float32
        ).astype(jnp.bfloat16),
        "fsdp",
        scatter_dimension=0,
        tiled=True,
    )
    grad_sum = lax.psum(shard_sum, "dp").astype(jnp.float32)
    entry_count = shard_rows * lax.axis_size("fsdp") * weight.shape[1]
    along_right = jnp.dot(grad_sum, right_next, precision=highest)
    grad_sq_raw, inner_prod, cross_term = lax.psum(
        (
            jnp.sum(grad_sum * grad_sum),
            jnp.sum(grad_sum * weight_wide),
            jnp.sum(left_next * along_right),
        ),
        "fsdp",
    )
    rank_coeff = inner_prod / (spectral * spectral)
    gradient = grad_sum / spectral - rank_coeff * left_next[:, None] * right_next[None, :]
    left_unit = left_sq / (left_sq + epsilon)
    right_unit = jnp.sum(right_next * right_next)
    grad_sq = (
        grad_sq_raw / (spectral * spectral)
        - 2.0 * rank_coeff * cross_term / spectral
        + rank_coeff * rank_coeff * left_unit * right_unit
    )
    grad_rms = jnp.sqrt(grad_sq / entry_count + epsilon)
    update = (gradient / grad_rms).astype(jnp.bfloat16)
    return (layer_out, input_grad, update, left_next, right_next)


def solution(mesh):
    placed = (P(("fsdp", "dp"), None), P(("fsdp", "dp"), None), P("fsdp", None), P("fsdp"))
    return jax.shard_map(
        per_device,
        mesh=mesh,
        in_specs=placed,
        out_specs=(
            P(("fsdp", "dp"), None),
            P(("fsdp", "dp"), None),
            P("fsdp", None),
            P("fsdp"),
            P(),
        ),
        check_vma=False,
    )
```

profile of v0, /device:TPU:0, one launch (start us, length us, event | category | flops | bytes accessed | tf_op | source)
XLA Modules:
  0.0 355.8 jit_solution(14946485540148376440)
XLA Ops:
  7.2 0.0 copy-start
  7.2 0.0 reduce-scatter.2.cloned.1.call-start
  7.2 1.5 copy-done
  8.8 14.6 %convolution_convert_fusion = bf16[4096,2048]{1,0:T(8,128)(2,1)} fusion(bf16[512,4096]{1,0:T(8,128)(2,1)} %param.4, bf16[512,2048]{1,0:T(8,128)(2,1)S(1)} %copy-done), kind=kOutput, calls=%fused_computation | convolution fusion | flops 8598323200 | bytes 23068672 | tf_op jit(solution)/shard_map/dot_general | solution.py:28
  23.4 0.0 reduce-scatter.2.cloned.1.call-update
  23.4 0.0 copy-start.3
  23.4 0.0 all-reduce.3.cloned.1.call-start
  23.5 119.0 %reduce-scatter.2.cloned.1.call-done = bf16[512,2048]{1,0:T(8,128)(2,1)} async-done(((bf16[4096,2048]{1,0:T(8,128)(2,1)}), bf16[512,2048]{1,0:T(8,128)(2,1)}) %reduce-scatter.2.cloned.1.call-update) | async-done | bytes 2097168 | tf_op jit(solution)/shard_map/reduce_scatter | solution.py:27
  142.5 0.0 all-reduce.3.cloned.1.call-update
  142.5 0.0 all-gather.2.cloned.1.call-start
  142.5 0.7 all-gather.2.cloned.1.call-update
  143.2 0.0 copy-done.3
  143.2 2.5 fusion.5
  145.7 13.2 %psum.42 = f32[2048]{0:T(1024)S(1)} all-reduce(f32[2048]{0:T(1024)S(1)} %bitcast.20), channel_id=1, replica_groups=mesh['fsdp'=8,'dp'=4] {'fsdp'}, use_global_device_ids=true, to_apply=%region_0.0 | all-reduce | flops 2048 | bytes 16384 | tf_op jit(solution)/shard_map/psum | solution.py:13
  158.9 0.6 multiply_reduce_fusion.1
  160.2 0.6 multiply_reduce_fusion
  160.8 0.0 copy-start.1
  160.8 3.3 fusion.6
  164.1 0.6 multiply_reduce_fusion.3
  164.7 13.2 %psum.43 = f32[]{:T(128)} all-reduce(f32[]{:T(128)} %multiply_reduce_fusion.3), channel_id=1, replica_groups=mesh['fsdp'=8,'dp'=4] {'fsdp'}, use_global_device_ids=true, to_apply=%region_3.0 | all-reduce | flops 1 | bytes 8 | tf_op jit(solution)/shard_map/psum | solution.py:16
  179.3 51.7 %all-reduce.3.cloned.1.call-done = bf16[512,2048]{1,0:T(8,128)(2,1)} async-done(((bf16[512,2048]{1,0:T(8,128)(2,1)}), bf16[512,2048]{1,0:T(8,128)(2,1)}) %all-reduce.3.cloned.1.call-update) | async-done | bytes 2097168 | tf_op jit(solution)/shard_map/psum | solution.py:35
  231.0 3.3 fusion.7
  234.3 0.6 multiply_reduce_fusion.2
  235.0 0.0 copy-start.2
  235.0 4.0 %fusion.2 = (f32[]{:T(128)}, f32[]{:T(128)}) fusion(bf16[512,2048]{1,0:T(8,128)(2,1)} %all-reduce.3.cloned.1.call-done, bf16[512,2048]{1,0:T(8,128)(2,1)} %param.6), kind=kLoop, calls=%fused_computation.7 | loop fusion | flops 6291454 | bytes 4194312 | tf_op jit(solution)/shard_map/reduce_sum | solution.py:41
  239.0 15.1 %all-reduce = (f32[]{:T(128)}, f32[]{:T(128)}, f32[]{:T(128)}) all-reduce(f32[]{:T(128)} %get-tuple-element.6, f32[]{:T(128)} %get-tuple-element.5, f32[]{:T(128)} %get-tuple-element.12), channel_id=1, replica_groups=mesh['fsdp'=8,'dp'=4] {'fsdp'}, use_global_device_ids=true, to_apply=%region_9.0 | all-reduce | flops 3 | bytes 24 | tf_op jit(solution)/shard_map/psum | solution.py:38
  256.8 0.0 copy-done.1
  256.8 3.7 %fusion.4 = bf16[512,2048]{1,0:T(8,128)(2,1)} fusion(bf16[512,2048]{1,0:T(8,128)(2,1)} %all-reduce.3.cloned.1.call-done, f32[]{:T(128)S(6)} %sqrt.11, f32[2048]{0:T(1024)S(1)} %get-tuple-element.11, f32[512]{0:T(512)S(1)} %broadcast_multiply_fusion, f32[]{:T(128)S(6)} %sqrt.10), kind=kLoop, calls=%fused_computation.9 | loop fusion | flops 6291456 | bytes 4204552 | tf_op jit(solution)/shard_map/convert_element_type | solution.py:56
  260.5 0.0 copy-done.2
  260.5 61.3 %all-gather.2.cloned.1.call-done = bf16[4096,2048]{1,0:T(8,128)(2,1)} async-done(((bf16[512,2048]{1,0:T(8,128)(2,1)}), bf16[4096,2048]{1,0:T(8,128)(2,1)}) %all-gather.2.cloned.1.call-update) | async-done | bytes 16777232 | tf_op jit(solution)/shard_map/all_gather | solution.py:19
  321.8 0.0 copy-start.4
  321.8 13.9 %divide_convert_fusion = bf16[512,4096]{1,0:T(8,128)(2,1)} fusion(bf16[512,2048]{1,0:T(8,128)(2,1)S(1)} %copy-done, bf16[4096,2048]{1,0:T(8,128)(2,1)} %all-gather.2.cloned.1.call-done, f32[]{:T(128)S(6)} %sqrt.10), kind=kOutput, calls=%fused_computation.1 | convolution fusion | flops 8594128896 | bytes 23068676 | tf_op jit(solution)/shard_map/dot_general | solution.py:22
  335.7 0.0 copy-done.4
  335.7 13.5 %divide_convert_fusion.1 = bf16[512,2048]{1,0:T(8,128)(2,1)} fusion(bf16[512,4096]{1,0:T(8,128)(2,1)S(1)} %copy-done.4, bf16[4096,2048]{1,0:T(8,128)(2,1)} %all-gather.2.cloned.1.call-done, f32[]{:T(128)S(6)} %sqrt.10), kind=kOutput, calls=%fused_computation.10 | convolution fusion | flops 8592031744 | bytes 23068676 | tf_op jit(solution)/shard_map/dot_general | solution.py:20
  (1 shorter events, 0.0 us)
Async XLA Ops:
  7.2 1.6 copy-start
  7.2 135.3 %reduce-scatter.2.cloned.1.call-start = ((), (), s32[]{:S(2)}) async-start(), calls=%async_computation.2 | async-start | bytes 18874368 | tf_op jit(solution)/shard_map/reduce_scatter | solution.py:27
  23.4 119.8 %copy-start.3 = (f32[512]{0:T(512)S(1)}, f32[512]{0:T(512)}, u32[]{:S(2)}) copy-start(f32[512]{0:T(512)} %param.7) | copy-start | bytes 6148
  23.4 207.6 %all-reduce.3.cloned.1.call-start = ((), (), s32[]{:S(2)}) async-start(), calls=%async_computation.3 | async-start | bytes 4194304 | tf_op jit(solution)/shard_map/psum | solution.py:35
  142.5 179.3 %all-gather.2.cloned.1.call-start = ((), (), s32[]{:S(2)}) async-start(), calls=%async_computation.1 | async-start | bytes 18874368 | tf_op jit(solution)/shard_map/all_gather | solution.py:19
  160.8 96.0 %copy-start.1 = (f32[2048]{0:T(1024)}, f32[2048]{0:T(1024)S(1)}, u32[]{:S(2)}) copy-start(f32[2048]{0:T(1024)S(1)} %get-tuple-element.11) | copy-start | bytes 24580
  235.0 25.5 %copy-start.2 = (f32[512]{0:T(512)}, f32[512]{0:T(512)S(1)}, u32[]{:S(2)}) copy-start(f32[512]{0:T(512)S(1)} %get-tuple-element.13) | copy-start | bytes 6148
  321.8 13.9 %copy-start.4 = (bf16[512,4096]{1,0:T(8,128)(2,1)S(1)}, bf16[512,4096]{1,0:T(8,128)(2,1)}, u32[]{:S(2)}) copy-start(bf16[512,4096]{1,0:T(8,128)(2,1)} %param.4) | copy-start | bytes 12582916
Sparse Core Ops, SparseCore 0:
  23.5 118.8 reduce-scatter.1
  144.8 86.1 all-reduce.2
  232.9 88.8 all-gather.1
where the time goes:
time: 356 us
  waiting for transfers between devices  233 us (65%)
  matrix products  51.2 us (14%)
  blocking collectives  41.4 us (12%)
  between operations  18.5 us (5%)
  other arithmetic  10.2 us (3%)
    reduce_scatter x1, waiting for transfers between devices, per_device(): lax.psum_scatter(lax.dot_general(tokens, cotangent, (((0,), (0,)), ((), (...  119 us
    all_gather x1, waiting for transfers between devices, per_device(): gathered = lax.all_gather(weight, 'fsdp', axis=0, tiled=True)  61.3 us
    psum x1, waiting for transfers between devices, per_device(): grad_sum = lax.psum(shard_sum, 'dp').astype(jnp.float32)  51.7 us
    psum x1, blocking collectives, per_device(): lax.psum((jnp.sum(grad_sum * grad_sum), jnp.sum(grad_sum * weight_wide),...  15.1 us
    dot_general x1, matrix products, per_device(): lax.dot_general(tokens, cotangent, (((0,), (0,)), ((), ())), preferred_el...  14.6 us
    dot_general x1, matrix products, per_device(): lax.dot_general(cotangent, gathered, (((1,), (1,)), ((), ())), preferred_...  13.9 us
    dot_general x1, matrix products, per_device(): product = jnp.dot(tokens, gathered, preferred_element_type=jnp.float32)  13.5 us
    psum x1, blocking collectives, per_device(): left_sq = lax.psum(jnp.sum(left_raw * left_raw), 'fsdp')  13.2 us
  transfers between devices with their start and end apart: 3, of which 3 were waited for; matrix products, arithmetic and copies ran while one was open for 5% of the time, Pallas kernels for 0%

commit v1 on v0

v1 whole, which is shorter than its diff:
```python
import functools

import jax
import jax.numpy as jnp
from jax import lax
from jax.experimental import pallas as pl
from jax.experimental.pallas import tpu as pltpu
from jax.sharding import PartitionSpec as P

epsilon = 1e-06


def swap(value, bit):
    size = lax.axis_size("fsdp")
    return lax.ppermute(value, "fsdp", [(i, i ^ (1 << bit)) for i in range(size)])


def total_kernel(part_ref, sum_ref, slots, send_sem, recv_sem):
    size = slots.shape[0]
    me = lax.axis_index("fsdp")
    barrier = pltpu.get_barrier_semaphore()
    for step in range(1, size):
        pl.semaphore_signal(
            barrier,
            inc=1,
            device_id={"fsdp": lax.rem(me + step, size)},
            device_id_type=pl.DeviceIdType.MESH,
        )
    pl.semaphore_wait(barrier, size - 1)

    def copy(step):
        return pltpu.make_async_remote_copy(
            src_ref=part_ref,
            dst_ref=slots.at[me],
            send_sem=send_sem.at[step],
            recv_sem=recv_sem.at[step],
            device_id={"fsdp": lax.rem(me + step, size)},
            device_id_type=pl.DeviceIdType.MESH,
        )

    for step in range(1, size):
        copy(step).start()
    slots[me] = part_ref[...]
    for step in range(1, size):
        copy(step).wait()
    sum_ref[...] = jnp.sum(slots[...], axis=0)


def total(part, collective_id):
    size = lax.axis_size("fsdp")
    return pl.pallas_call(
        total_kernel,
        out_shape=jax.ShapeDtypeStruct(part.shape, part.dtype),
        in_specs=[pl.BlockSpec(memory_space=pltpu.VMEM)],
        out_specs=pl.BlockSpec(memory_space=pltpu.VMEM),
        scratch_shapes=[
            pltpu.VMEM((size, *part.shape), part.dtype),
            pltpu.SemaphoreType.DMA((size,)),
            pltpu.SemaphoreType.DMA((size,)),
        ],
        compiler_params=pltpu.CompilerParams(collective_id=collective_id, has_side_effects=True),
        cost_estimate=pl.CostEstimate(flops=0, bytes_accessed=2**22, transcendentals=0),
    )(part)


def lanes(*scalars):
    rows = jnp.arange(8)[:, None]
    return sum(jnp.where(rows == i, s, 0.0) for i, s in enumerate(scalars)) + jnp.zeros((8, 128))


def replica_sum(part, group):
    size = lax.axis_size("dp")
    me = lax.axis_index("dp")
    order = list(range(size.bit_length() - 1))
    if group % 2 == 1:
        order.reverse()

    def across(value, bit):
        return lax.ppermute(value, "dp", [(i, i ^ (1 << bit)) for i in range(size)])

    for bit in order:
        mine = jnp.bitwise_and(jnp.right_shift(me, bit), 1)
        rows = part.shape[0] // 2
        kept = lax.dynamic_slice_in_dim(part, mine * rows, rows, axis=0)
        sent = lax.dynamic_slice_in_dim(part, (1 - mine) * rows, rows, axis=0)
        part = kept + across(sent.astype(jnp.bfloat16), bit).astype(jnp.float32)
    part = part.astype(jnp.bfloat16)
    for bit in reversed(order):
        mine = jnp.bitwise_and(jnp.right_shift(me, bit), 1)
        other = across(part, bit)
        low = jnp.where(mine == 0, part, other)
        high = jnp.where(mine == 0, other, part)
        part = jnp.concatenate([low, high], axis=0)
    return part


def project_kernel(base, count, first, last, *refs):
    scale_ref, tokens, cotangent = refs[:3]
    pieces = refs[3 : 3 + 2 * count]
    rest = list(refs[3 + 2 * count :])
    if not first:
        acc_in, _ = rest[:2]
        rest = rest[2:]
    out_ref, back_ref = rest[:2]
    tok_v, cot_v, w_v, back_v, acc, tok_sem, w_sem, back_sem, cot_sem = rest[2:11]
    me = lax.axis_index("fsdp")
    half, _ = pieces[0].shape
    rows = 2 * half

    def columns(k):
        start = jnp.bitwise_xor(me, base + k) * rows
        return pl.ds(pl.multiple_of(start, rows), rows)

    def load_tok(k):
        return pltpu.make_async_copy(tokens.at[:, columns(k)], tok_v.at[k], tok_sem.at[k])

    def load_w(piece, k, side):
        return pltpu.make_async_copy(
            piece, w_v.at[k, pl.ds(side * half, half)], w_sem.at[k, side]
        )

    def store_back(k):
        return pltpu.make_async_copy(back_v.at[k], back_ref.at[:, columns(k)], back_sem.at[k])

    load_cot = pltpu.make_async_copy(cotangent, cot_v, cot_sem.at[0])
    for k in range(count):
        load_tok(k).start()
        for side in (0, 1):
            load_w(pieces[2 * k + side], k, side).start()
        if k == 0:
            load_cot.start()
    if first:
        acc[...] = jnp.zeros_like(acc)
    else:
        load_acc = pltpu.make_async_copy(acc_in, acc, cot_sem.at[1])
        load_acc.start()
        load_acc.wait()
    load_cot.wait()
    scale = scale_ref[0]

    @pl.loop(0, count)
    def _(k):
        load_tok(k).wait()
        load_w(pieces[0], k, 0).wait()
        load_w(pieces[1], k, 1).wait()
        acc[...] += jnp.dot(tok_v[k], w_v[k], preferred_element_type=jnp.float32)
        back = lax.dot_general(
            cot_v[...], w_v[k], (((1,), (1,)), ((), ())), preferred_element_type=jnp.float32
        )
        back_v[k] = (back * scale).astype(back_v.dtype)
        store_back(k).start()

    if last:
        out_ref[...] = (acc[...] * scale).astype(out_ref.dtype)
    else:
        out_ref[...] = acc[...]

    @pl.loop(0, count)
    def _(k):
        store_back(k).wait()


def project(scale, tokens, cotangent, pieces, base, carry, last):
    count = len(pieces) // 2
    toks, width = tokens.shape
    outs = cotangent.shape[1]
    rows = 2 * pieces[0].shape[0]
    any_space = pl.BlockSpec(memory_space=pl.ANY)
    first = carry is None
    operands = [scale, tokens, cotangent, *pieces] + ([] if first else list(carry))
    in_specs = [pl.BlockSpec(memory_space=pltpu.SMEM)] + [any_space] * (len(operands) - 1)
    return pl.pallas_call(
        functools.partial(project_kernel, base, count, first, last),
        out_shape=(
            jax.ShapeDtypeStruct((toks, outs), jnp.bfloat16 if last else jnp.float32),
            jax.ShapeDtypeStruct((toks, width), jnp.bfloat16),
        ),
        in_specs=in_specs,
        out_specs=(pl.BlockSpec(memory_space=pltpu.VMEM), any_space),
        scratch_shapes=[
            pltpu.VMEM((count, toks, rows), jnp.bfloat16),
            pltpu.VMEM((toks, outs), jnp.bfloat16),
            pltpu.VMEM((count, rows, outs), jnp.bfloat16),
            pltpu.VMEM((count, toks, rows), jnp.bfloat16),
            pltpu.VMEM((toks, outs), jnp.float32),
            pltpu.SemaphoreType.DMA((count,)),
            pltpu.SemaphoreType.DMA((count, 2)),
            pltpu.SemaphoreType.DMA((count,)),
            pltpu.SemaphoreType.DMA((2,)),
        ],
        input_output_aliases={} if first else {len(operands) - 1: 1},
        compiler_params=pltpu.CompilerParams(vmem_limit_bytes=56 * 2**20),
        cost_estimate=pl.CostEstimate(
            flops=4 * count * rows * toks * outs,
            bytes_accessed=2 * count * rows * (outs + 2 * toks) + 4 * toks * outs,
            transcendentals=0,
        ),
    )(*operands)


def step(tokens, cotangent, weight, left_vector):
    highest = lax.Precision.HIGHEST
    wide, narrow = jnp.float32, jnp.bfloat16
    size = lax.axis_size("fsdp")
    bits = size.bit_length() - 1
    me = lax.axis_index("fsdp")
    shard_rows, outs = weight.shape
    half = shard_rows // 2
    orders = (tuple(range(1, bits)), tuple(range(bits - 1, 0, -1)))

    def token_block(rel):
        start = jnp.bitwise_xor(me, rel) * shard_rows
        return lax.dynamic_slice_in_dim(tokens, start, shard_rows, axis=1)

    evens = [rel for rel in range(size) if rel % 2 == 0]
    cot_chip = jnp.concatenate([cotangent, swap(cotangent, 0)], axis=0)
    tok_chip = {
        rel: jnp.concatenate([token_block(rel), swap(token_block(rel | 1), 0)], axis=0)
        for rel in reversed(evens)
    }

    weight_wide = weight.astype(wide)
    part_right = jnp.dot(left_vector, weight_wide, precision=highest)
    right_raw = total(part_right.reshape(outs // 128, 128), 1).reshape(outs)
    right_next = right_raw / jnp.sqrt(jnp.sum(right_raw * right_raw) + epsilon)
    left_raw = jnp.dot(weight_wide, right_next, precision=highest)
    left_sq = total(lanes(jnp.sum(left_raw * left_raw)), 2)[0, 0]
    spectral = jnp.sqrt(left_sq + epsilon)
    left_next = left_raw / spectral

    sides = (0, 1)
    cot_chip, tok_chip, left_sq = lax.optimization_barrier((cot_chip, tok_chip, left_sq))

    groups = 2
    group_cols = outs // groups
    live = {}
    for group in range(groups):
        cot_part = cot_chip[:, group * group_cols : (group + 1) * group_cols]
        for side in sides:
            live[group, side] = {
                rel: lax.dot_general(
                    tok_chip[rel][:, side * half : (side + 1) * half],
                    cot_part,
                    (((0,), (0,)), ((), ())),
                    preferred_element_type=wide,
                ).astype(narrow)
                for rel in reversed(evens)
            }
    for phase in range(bits - 1):
        for group in range(groups):
            for side in sides:
                mask = 1 << orders[side][phase]
                now = live[group, side]
                live[group, side] = {
                    rel: now[rel].astype(wide)
                    + swap(now[rel | mask].astype(narrow), orders[side][phase]).astype(wide)
                    for rel in sorted(now)
                    if not rel & mask
                }
    grad_parts = [
        replica_sum(
            jnp.concatenate([live[group, side][0] for side in sides], axis=0), group
        )
        for group in range(groups)
    ]
    grad_sum = jnp.concatenate(grad_parts, axis=1).astype(wide)

    own_a, own_b, _ = lax.optimization_barrier(
        (weight[:half], weight[half:], [live[0, side][0] for side in sides])
    )
    held = ({0: own_a}, {0: own_b})
    for side in sides:
        for bit in orders[side]:
            for rel in sorted(held[side]):
                held[side][rel | (1 << bit)] = swap(held[side][rel], bit)
    for side in sides:
        for rel in sorted(held[side]):
            held[side][rel | 1] = swap(held[side][rel], 0)

    entry_count = shard_rows * size * outs
    outer = left_next[:, None] * right_next[None, :]
    sums = total(
        lanes(
            jnp.sum(grad_sum * grad_sum),
            jnp.sum(grad_sum * weight_wide),
            jnp.sum(grad_sum * outer),
        ),
        3,
    )
    grad_sq_raw, inner_prod, cross_term = sums[0, 0], sums[1, 0], sums[2, 0]
    rank_coeff = inner_prod / (spectral * spectral)
    gradient = grad_sum / spectral - rank_coeff * outer
    left_unit = left_sq / (left_sq + epsilon)
    right_unit = jnp.sum(right_next * right_next)
    grad_sq = (
        grad_sq_raw / (spectral * spectral)
        - 2.0 * rank_coeff * cross_term / spectral
        + rank_coeff * rank_coeff * left_unit * right_unit
    )
    grad_rms = jnp.sqrt(grad_sq / entry_count + epsilon)
    update = (gradient / grad_rms).astype(narrow)

    scale = (1.0 / spectral).reshape(1)
    near, far = range(size - 2), range(size - 2, size)
    halves = lambda rels: [held[side][rel] for rel in rels for side in (0, 1)]
    carry = project(scale, tokens, cotangent, halves(near), 0, None, False)
    layer_out, input_grad = project(scale, tokens, cotangent, halves(far), size - 2, carry, True)
    return (layer_out, input_grad, update, left_next, right_next)


def solution(mesh):
    placed = (P(("fsdp", "dp"), None), P(("fsdp", "dp"), None), P("fsdp", None), P("fsdp"))
    return jax.shard_map(
        step,
        mesh=mesh,
        in_specs=placed,
        out_specs=(
            P(("fsdp", "dp"), None),
            P(("fsdp", "dp"), None),
            P("fsdp", None),
            P("fsdp"),
            P(),
        ),
        check_vma=False,
    )
```

time: 356 us -> 299 us (0.84)
  waiting for transfers between devices: 233 us -> 130 us
  Pallas kernels: 0 us -> 54.9 us
  blocking collectives: 41.4 us -> 0 us
  matrix products: 51.2 us -> 15 us
  starting transfers between devices: 0.12 us -> 33.9 us
  other arithmetic: 10.2 us -> 41 us
  local copies, waits for them, and re-layouts: 1.56 us -> 16.2 us
  between operations: 18.5 us -> 6.43 us
    ppermute x0 -> x39, waiting for transfers between devices: none -> 130 us  [the longest x31 91.2 us: swap(): return lax.ppermute(value, 'fsdp', [(i, i ^ 1 << bit) for i in range(size)])]
    reduce_scatter x1 -> x0, waiting for transfers between devices: 119 us -> none  [per_device(): lax.psum_scatter(lax.dot_general(tokens, cotangent, (((0,), (0,)), ((), (...]
    all_gather x1 -> x0, waiting for transfers between devices: 61.3 us -> none  [per_device(): gathered = lax.all_gather(weight, 'fsdp', axis=0, tiled=True)]
    pallas_call x0 -> x5, Pallas kernels: none -> 54.9 us  [the longest x2 34.6 us: project(): pl.pallas_call(functools.partial(project_kernel, base, count, first, last...]
    psum x1 -> x0, waiting for transfers between devices: 51.7 us -> none  [per_device(): grad_sum = lax.psum(shard_sum, 'dp').astype(jnp.float32)]
    psum x3 -> x0, blocking collectives: 41.4 us -> none  [the longest x1 15.1 us: per_device(): lax.psum((jnp.sum(grad_sum * grad_sum), jnp.sum(grad_sum * weight_wide),...]
    dot_general x6 -> x18, matrix products: 51.2 us -> 15 us  [the longest x16 11.8 us: step(): lax.dot_general(tok_chip[rel][:, side * half:(side + 1) * half], cot_part...]
    ppermute x0 -> x39, starting transfers between devices: none -> 33.9 us  [the longest x31 25.5 us: swap(): return lax.ppermute(value, 'fsdp', [(i, i ^ 1 << bit) for i in range(size)])]
  transfers between devices with their start and end apart: 3 -> 39, of which waited for: 3 -> 15; matrix products, arithmetic and copies ran while one was open for 5% -> 19% of each run, Pallas kernels for 0% -> 15%
where the time goes in v1:
time: 299 us; the launch traced here: 298 us
  waiting for transfers between devices  130 us (43%)
  Pallas kernels  54.9 us (18%)
  other arithmetic  41 us (14%)
  starting transfers between devices  33.9 us (11%)
  local copies, waits for them, and re-layouts  16.2 us (5%)
  matrix products  15 us (5%)
  between operations  6.43 us (2%)
    ppermute x31, waiting for transfers between devices, swap(): return lax.ppermute(value, 'fsdp', [(i, i ^ 1 << bit) for i in range(size)])  91.2 us
    ppermute x8, waiting for transfers between devices, across(): return lax.ppermute(value, 'dp', [(i, i ^ 1 << bit) for i in range(size)])  39.2 us
    pallas_call x2, Pallas kernels, project(): pl.pallas_call(functools.partial(project_kernel, base, count, first, last...  34.6 us
    ppermute x31, starting transfers between devices, swap(): return lax.ppermute(value, 'fsdp', [(i, i ^ 1 << bit) for i in range(size)])  25.5 us
    pallas_call x3, Pallas kernels, total(): pl.pallas_call(total_kernel, out_shape=jax.ShapeDtypeStruct(part.shape, p...  20.3 us
    dot_general x16, matrix products, step(): lax.dot_general(tok_chip[rel][:, side * half:(side + 1) * half], cot_part...  11.8 us
    reduce_sum x1, other arithmetic, step(): jnp.sum(grad_sum * grad_sum)  9.54 us
    ppermute x8, starting transfers between devices, across(): return lax.ppermute(value, 'dp', [(i, i ^ 1 << bit) for i in range(size)])  8.44 us
  transfers between devices with their start and end apart: 39, of which 15 were waited for; matrix products, arithmetic and copies ran while one was open for 19% of the time, Pallas kernels for 15%

profile of v1, /device:TPU:0, one launch (start us, length us, event | category | flops | bytes accessed | tf_op | source)
XLA Modules:
  0.0 297.9 jit_solution(3555847508894449507)
XLA Ops:
  1.2 4.0 %constant_dynamic-slice_fusion.1 = (bf16[512,512]{1,0:T(8,128)(2,1)S(1)}, bf16[512,512]{1,0:T(8,128)(2,1)}, bf16[512,512]{1,0:T(8,128)(2,1)}, bf16[512,512]{1,0:...) fusion(bf16[512,4096]{1,0:T(8,128)(2,1)} %refs_1_.3, ...), kind=kLoop, calls=%fused_computation.114 | loop fusion | bytes 8388640 | tf_op jit(solution)/shard_map/dynamic_slice | solution.py:213
  6.3 1.5 fusion.66
  7.8 7.4 %shard_map.83 = f32[16,128]{1,0:T(8,128)} custom-call(f32[16,128]{1,0:T(8,128)} %bitcast.22), custom_call_target="tpu_custom_call" | custom-call | bytes 4194304 | tf_op jit(solution)/shard_map/pallas_call | solution.py:51
  15.1 1.3 multiply_reduce_fusion.1
  17.1 1.3 multiply_reduce_fusion
  18.4 1.7 fusion.67
  22.1 6.0 %shard_map.84 = f32[8,128]{1,0:T(8,128)} custom-call(f32[8,128]{1,0:T(8,128)} %add.138.part_ref), custom_call_target="tpu_custom_call" | custom-call | bytes 4194304 | tf_op jit(solution)/shard_map/pallas_call | solution.py:51
  28.1 1.2 slice.56
  29.3 1.4 pad_maximum_fusion.1
  30.7 1.3 pad_maximum_fusion.2
  32.0 1.1 pad_maximum_fusion.3
  33.1 1.1 pad_maximum_fusion.4
  34.3 2.6 pad_maximum_fusion
  43.5 1.5 collective-permute-start.8
  46.3 1.5 collective-permute-start.5
  48.4 1.5 collective-permute-start.33
  51.3 18.3 %collective-permute-done.9 = bf16[256,1024]{1,0:T(8,128)(2,1)S(1)} collective-permute-done((bf16[256,1024]{1,0:T(8,128)(2,1)S(1)}, bf16[256,1024]{1,0:T(8,128)(2,1)S(1)}, u32[]{:S(2)}, u32[]{:S(2)}) %collective-permute-start.9) | collective-permute-done | bytes 524320 | tf_op jit(solution)/shard_map/ppermute | solution.py:15
  69.6 1.5 collective-permute-start.32
  71.8 1.5 collective-permute-start.30
  74.0 6.8 %collective-permute-done.33 = bf16[256,1024]{1,0:T(8,128)(2,1)S(1)} collective-permute-done((bf16[256,1024]{1,0:T(8,128)(2,1)S(1)}, bf16[256,1024]{1,0:T(8,128)(2,1)S(1)}, u32[]{:S(2)}, u32[]{:S(2)}) %collective-permute-start.33) | collective-permute-done | bytes 524320 | tf_op jit(solution)/shard_map/ppermute | solution.py:15
  80.8 1.5 collective-permute-start.10
  83.2 2.7 collective-permute-done.30
  87.4 1.5 collective-permute-start.29
  89.0 8.1 %collective-permute-done.10 = bf16[256,1024]{1,0:T(8,128)(2,1)S(1)} collective-permute-done((bf16[256,1024]{1,0:T(8,128)(2,1)S(1)}, bf16[256,1024]{1,0:T(8,128)(2,1)S(1)}, u32[]{:S(2)}, u32[]{:S(2)}) %collective-permute-start.10) | collective-permute-done | bytes 524320 | tf_op jit(solution)/shard_map/ppermute | solution.py:15
  97.1 1.4 collective-permute-start.34
  98.8 0.9 collective-permute-start.31
  99.7 3.6 %collective-permute-done.7 = bf16[256,1024]{1,0:T(8,128)(2,1)S(1)} collective-permute-done((bf16[256,1024]{1,0:T(8,128)(2,1)S(1)}, bf16[256,1024]{1,0:T(8,128)(2,1)S(1)}, u32[]{:S(2)}, u32[]{:S(2)}) %collective-permute-start.7) | collective-permute-done | bytes 524320 | tf_op jit(solution)/shard_map/ppermute | solution.py:15
  103.5 1.1 fusion.19
  104.7 1.6 collective-permute-start.25
  106.2 11.3 %collective-permute-done.34 = bf16[256,1024]{1,0:T(8,128)(2,1)S(1)} collective-permute-done((bf16[256,1024]{1,0:T(8,128)(2,1)S(1)}, bf16[256,1024]{1,0:T(8,128)(2,1)S(1)}, u32[]{:S(2)}, u32[]{:S(2)}) %collective-permute-start.34) | collective-permute-done | bytes 524320 | tf_op jit(solution)/shard_map/ppermute | solution.py:15
  118.0 1.2 fusion.15
  119.3 2.5 collective-permute-start.35
  121.8 1.8 fusion.21
  124.1 26.3 %collective-permute-done.35 = bf16[256,1024]{1,0:T(8,128)(2,1)} collective-permute-done((bf16[256,1024]{1,0:T(8,128)(2,1)}, bf16[256,1024]{1,0:T(8,128)(2,1)}, u32[]{:S(2)}, u32[]{:S(2)}) %collective-permute-start.35) | collective-permute-done | bytes 524320 | tf_op jit(solution)/shard_map/ppermute | solution.py:79
  150.4 1.4 fusion.17
  152.5 2.4 collective-permute-done.26
  155.8 1.6 fusion.64
  157.4 1.4 collective-permute-start.11
  159.4 5.4 %collective-permute-done.36 = bf16[128,1024]{1,0:T(8,128)(2,1)} collective-permute-done((bf16[128,1024]{1,0:T(8,128)(2,1)}, bf16[128,1024]{1,0:T(8,128)(2,1)}, u32[]{:S(2)}, u32[]{:S(2)}) %collective-permute-start.36) | collective-permute-done | bytes 262176 | tf_op jit(solution)/shard_map/ppermute | solution.py:79
  164.8 1.0 add_convert_fusion.4
  165.9 3.1 %collective-permute-done.27 = bf16[128,1024]{1,0:T(8,128)(2,1)} collective-permute-done((bf16[128,1024]{1,0:T(8,128)(2,1)S(1)}, bf16[128,1024]{1,0:T(8,128)(2,1)}, u32[]{:S(2)}, u32[]{:S(2)}) %collective-permute-start.27) | collective-permute-done | bytes 262176 | tf_op jit(solution)/shard_map/ppermute | solution.py:79
  169.1 1.1 broadcast_select_fusion.7
  171.7 1.0 collective-permute-start.28
  172.7 2.0 collective-permute-done.37
  176.2 2.0 collective-permute-start.38
  180.0 1.3 collective-permute-start.22
  181.4 2.4 collective-permute-done.11.refs_7_
  183.8 1.3 collective-permute-start.13
  185.1 19.5 %collective-permute-done.19.refs_8_ = bf16[256,2048]{1,0:T(8,128)(2,1)} collective-permute-done((bf16[256,2048]{1,0:T(8,128)(2,1)}, bf16[256,2048]{1,0:T(8,128)(2,1)}, u32[]{:S(2)}, u32[]{:S(2)}) %collective-permute-start.19) | collective-permute-done | bytes 1048608 | tf_op jit(solution)/shard_map/ppermute | solution.py:15
  206.7 1.4 broadcast_select_fusion.3
  208.1 1.4 broadcast_select_fusion.1
  209.6 9.5 %fusion.3 = (f32[]{:T(128)}, f32[]{:T(128)}, f32[]{:T(128)}) fusion(bf16[256,1024]{1,0:T(8,128)(2,1)S(1)} %get-tuple-element.47, bf16[256,1024]{1,0:T(8,128)(2,1)S(1)} %get-tuple-element.46, bf16[256,1024]{1,0:T(8,128)(2,1)S(1)} %get-tuple-element.45, bf16[256,1024]{1,0:T(8,128)(2,1)S(1)} %get-tuple-element.44, f32[2048]{0:T(1024)S(1)} %bitcast.19, ...), kind=kLoop, calls=%fused_computation.8 | loop fusion | flops 16777213 | bytes 4204556 | tf_op jit(solution)/shard_map/reduce_sum | solution.py:284
  219.1 1.9 fusion.63
  221.7 7.0 %shard_map.87 = f32[8,128]{1,0:T(8,128)} custom-call(f32[8,128]{1,0:T(8,128)} %add.174.part_ref), custom_call_target="tpu_custom_call" | custom-call | bytes 4194304 | tf_op jit(solution)/shard_map/pallas_call | solution.py:51
  228.6 1.4 fusion.65
  232.6 1.3 collective-permute-start.12
  233.9 1.5 collective-permute-start.14
  236.0 5.2 %fusion.2 = bf16[512,2048]{1,0:T(8,128)(2,1)} fusion(f32[]{:T(128)S(6)} %sqrt.11, f32[]{:T(128)S(6)} %div.58, f32[2048]{0:T(1024)S(1)} %bitcast.20, f32[512]{0:T(512)S(1)} %broadcast_divide_fusion.1, f32[]{:T(128)S(6)} %sqrt.10, bf16[256,1024]{1,0:T(8,128)(2,1)} %copy-done.10, bf16[256,1024]{1,0:T(8,128)(2,1)} %copy-done.9, ...), kind=kLoop, calls=%fused_computation.7 | loop fusion | flops 14680064 | bytes 4204556 | tf_op jit(solution)/shard_map/convert_element_type | solution.py:301
  241.2 16.8 %collective-permute-done.12.refs_3_ = bf16[256,2048]{1,0:T(8,128)(2,1)S(1)} collective-permute-done((bf16[256,2048]{1,0:T(8,128)(2,1)}, bf16[256,2048]{1,0:T(8,128)(2,1)S(1)}, u32[]{:S(2)}, u32[]{:S(2)}) %collective-permute-start.12) | collective-permute-done | bytes 1048608 | tf_op jit(solution)/shard_map/ppermute | solution.py:15
  258.0 1.7 collective-permute-done.14.refs_4_
  259.8 1.0 copy-done.25
  261.8 23.2 %shard_map.85 = (f32[512,2048]{1,0:T(8,128)}, bf16[512,4096]{1,0:T(8,128)(2,1)}) custom-call(f32[1]{0:T(128)} %bitcast.7.refs_0_, bf16[512,4096]{1,0:T(8,128)(2,1)} %refs_1_.3, bf16[512,2048]{1,0:T(8,128)(2,1)} %refs_2_.3, bf16[256,2048]{1,0:T(8,128)(2,1)} %get-tuple-element.22.refs_3_, bf16[256,2048]{1,0:T(8,128)(2,1)} %get-tuple-element.23.refs_4_, ...), custom_call_target="tpu_custom_call" | custom-call | flops 12884901888 | bytes 23068672 | tf_op jit(solution)/shard_map/pallas_call | solution.py:172
  285.0 1.0 copy-done.17
  286.4 11.4 %shard_map.86 = (bf16[512,2048]{1,0:T(8,128)(2,1)}, bf16[512,4096]{1,0:T(8,128)(2,1)}) custom-call(f32[1]{0:T(128)} %bitcast.7.refs_0_, bf16[512,4096]{1,0:T(8,128)(2,1)} %refs_1_.3, bf16[512,2048]{1,0:T(8,128)(2,1)} %refs_2_.3, bf16[256,2048]{1,0:T(8,128)(2,1)} %copy-done.15, bf16[256,2048]{1,0:T(8,128)(2,1)} %copy-done.16, ...), custom_call_target="tpu_custom_call", output_to_operand_aliasing={{1}: (8, {})} | custom-call | flops 4294967296 | bytes 10485760 | tf_op jit(solution)/shard_map/pallas_call | solution.py:172
  (126 shorter events, 28.9 us)
Async XLA Ops:
  0.6 5.6 %copy-start = (f32[512]{0:T(512)S(1)}, f32[512]{0:T(512)}, u32[]{:S(2)}) copy-start(f32[512]{0:T(512)} %param.7) | copy-start | bytes 6148
  0.6 33.6 %collective-permute-start = (bf16[512,2048]{1,0:T(8,128)(2,1)}, bf16[512,2048]{1,0:T(8,128)(2,1)}, u32[]{:S(2)}, u32[]{:S(2)}) collective-permute-start(bf16[512,2048]{1,0:T(8,128)(2,1)} %refs_2_.3), channel_id=1, source_target_pairs={{0,4},{4,0},{8,12},{12,8},{16,20},{20,16},{24,28},{28,24},{1,5},{5... | collective-permute-start | bytes 6291464 | tf_op jit(solution)/shard_map/ppermute | solution.py:15
  1.2 5.0 %copy-start.2 = (bf16[512,2048]{1,0:T(8,128)(2,1)S(1)}, bf16[512,2048]{1,0:T(8,128)(2,1)}, u32[]{:S(2)}) copy-start(bf16[512,2048]{1,0:T(8,128)(2,1)} %param.6) | copy-start | bytes 6291460
  5.2 24.1 %collective-permute-start.1 = (bf16[512,512]{1,0:T(8,128)(2,1)}, bf16[512,512]{1,0:T(8,128)(2,1)}, u32[]{:S(2)}, u32[]{:S(2)}) collective-permute-start(bf16[512,512]{1,0:T(8,128)(2,1)} %get-tuple-element.40), channel_id=1, source_target_pairs={{0,4},{4,0},{8,12},{12,8},{16,20},{20,16},{24,28},{28,24},{1,5},{5... | collective-permute-start | bytes 1572872 | tf_op jit(solution)/shard_map/ppermute | solution.py:15
  5.3 25.4 %collective-permute-start.2 = (bf16[512,512]{1,0:T(8,128)(2,1)}, bf16[512,512]{1,0:T(8,128)(2,1)}, u32[]{:S(2)}, u32[]{:S(2)}) collective-permute-start(bf16[512,512]{1,0:T(8,128)(2,1)} %get-tuple-element.38), channel_id=1, source_target_pairs={{0,4},{4,0},{8,12},{12,8},{16,20},{20,16},{24,28},{28,24},{1,5},{5... | collective-permute-start | bytes 1572872 | tf_op jit(solution)/shard_map/ppermute | solution.py:15
  5.7 26.3 %collective-permute-start.3 = (bf16[512,512]{1,0:T(8,128)(2,1)}, bf16[512,512]{1,0:T(8,128)(2,1)}, u32[]{:S(2)}, u32[]{:S(2)}) collective-permute-start(bf16[512,512]{1,0:T(8,128)(2,1)} %get-tuple-element.36), channel_id=1, source_target_pairs={{0,4},{4,0},{8,12},{12,8},{16,20},{20,16},{24,28},{28,24},{1,5},{5... | collective-permute-start | bytes 1572872 | tf_op jit(solution)/shard_map/ppermute | solution.py:15
  5.8 27.3 %collective-permute-start.4 = (bf16[512,512]{1,0:T(8,128)(2,1)}, bf16[512,512]{1,0:T(8,128)(2,1)}, u32[]{:S(2)}, u32[]{:S(2)}) collective-permute-start(bf16[512,512]{1,0:T(8,128)(2,1)} %get-tuple-element.35), channel_id=1, source_target_pairs={{0,4},{4,0},{8,12},{12,8},{16,20},{20,16},{24,28},{28,24},{1,5},{5... | collective-permute-start | bytes 1572872 | tf_op jit(solution)/shard_map/ppermute | solution.py:15
  18.4 217.5 %copy-start.21 = (f32[16,128]{1,0:T(8,128)}, f32[16,128]{1,0:T(8,128)S(1)}, u32[]{:S(2)}) copy-start(f32[16,128]{1,0:T(8,128)S(1)} %get-tuple-element.33) | copy-start | bytes 24580
  29.3 5.0 %copy-start.8 = (bf16[512,2048]{1,0:T(8,128)(2,1)S(1)}, bf16[512,2048]{1,0:T(8,128)(2,1)}, u32[]{:S(2)}) copy-start(bf16[512,2048]{1,0:T(8,128)(2,1)} %refs_2_.3) | copy-start | bytes 6291460
  43.5 44.0 %collective-permute-start.8 = (bf16[256,1024]{1,0:T(8,128)(2,1)S(1)}, bf16[256,1024]{1,0:T(8,128)(2,1)S(1)}, u32[]{:S(2)}, u32[]{:S(2)}) collective-permute-start(bf16[256,1024]{1,0:T(8,128)(2,1)S(1)} %convolution_convert_fusion.10), channel_id=1, source_target_pairs={{0,16},{4,20},{8,24},{12,28},{16,0},{20,4},{24,8},{28,12},{1,17},{... | collective-permute-start | bytes 1572872 | tf_op jit(solution)/shard_map/ppermute | solution.py:15
  45.0 24.6 %collective-permute-start.9 = (bf16[256,1024]{1,0:T(8,128)(2,1)S(1)}, bf16[256,1024]{1,0:T(8,128)(2,1)S(1)}, u32[]{:S(2)}, u32[]{:S(2)}) collective-permute-start(bf16[256,1024]{1,0:T(8,128)(2,1)S(1)} %convolution_convert_fusion.8), channel_id=1, source_target_pairs={{0,16},{4,20},{8,24},{12,28},{16,0},{20,4},{24,8},{28,12},{1,17},{... | collective-permute-start | bytes 1572872 | tf_op jit(solution)/shard_map/ppermute | solution.py:15
  46.3 52.5 %collective-permute-start.5 = (bf16[256,1024]{1,0:T(8,128)(2,1)S(1)}, bf16[256,1024]{1,0:T(8,128)(2,1)S(1)}, u32[]{:S(2)}, u32[]{:S(2)}) collective-permute-start(bf16[256,1024]{1,0:T(8,128)(2,1)S(1)} %convolution_convert_fusion.14), channel_id=1, source_target_pairs={{0,8},{4,12},{8,0},{12,4},{16,24},{20,28},{24,16},{28,20},{1,9},{5... | collective-permute-start | bytes 1572872 | tf_op jit(solution)/shard_map/ppermute | solution.py:15
  47.8 23.9 %collective-permute-start.6 = (bf16[256,1024]{1,0:T(8,128)(2,1)S(1)}, bf16[256,1024]{1,0:T(8,128)(2,1)S(1)}, u32[]{:S(2)}, u32[]{:S(2)}) collective-permute-start(bf16[256,1024]{1,0:T(8,128)(2,1)S(1)} %convolution_convert_fusion.12), channel_id=1, source_target_pairs={{0,8},{4,12},{8,0},{12,4},{16,24},{20,28},{24,16},{28,20},{1,9},{5... | collective-permute-start | bytes 1572872 | tf_op jit(solution)/shard_map/ppermute | solution.py:15
  48.4 32.4 %collective-permute-start.33 = (bf16[256,1024]{1,0:T(8,128)(2,1)S(1)}, bf16[256,1024]{1,0:T(8,128)(2,1)S(1)}, u32[]{:S(2)}, u32[]{:S(2)}) collective-permute-start(bf16[256,1024]{1,0:T(8,128)(2,1)S(1)} %convolution_convert_fusion), channel_id=1, source_target_pairs={{0,16},{4,20},{8,24},{12,28},{16,0},{20,4},{24,8},{28,12},{1,17},{... | collective-permute-start | bytes 1572872 | tf_op jit(solution)/shard_map/ppermute | solution.py:15
  69.6 36.7 %collective-permute-start.32 = (bf16[256,1024]{1,0:T(8,128)(2,1)S(1)}, bf16[256,1024]{1,0:T(8,128)(2,1)S(1)}, u32[]{:S(2)}, u32[]{:S(2)}) collective-permute-start(bf16[256,1024]{1,0:T(8,128)(2,1)S(1)} %convolution_convert_fusion.2), channel_id=1, source_target_pairs={{0,16},{4,20},{8,24},{12,28},{16,0},{20,4},{24,8},{28,12},{1,17},{... | collective-permute-start | bytes 1572872 | tf_op jit(solution)/shard_map/ppermute | solution.py:15
  71.8 14.1 %collective-permute-start.30 = (bf16[256,1024]{1,0:T(8,128)(2,1)S(1)}, bf16[256,1024]{1,0:T(8,128)(2,1)S(1)}, u32[]{:S(2)}, u32[]{:S(2)}) collective-permute-start(bf16[256,1024]{1,0:T(8,128)(2,1)S(1)} %convolution_convert_fusion.4), channel_id=1, source_target_pairs={{0,8},{4,12},{8,0},{12,4},{16,24},{20,28},{24,16},{28,20},{1,9},{5... | collective-permute-start | bytes 1572872 | tf_op jit(solution)/shard_map/ppermute | solution.py:15
  80.8 16.3 %collective-permute-start.10 = (bf16[256,1024]{1,0:T(8,128)(2,1)S(1)}, bf16[256,1024]{1,0:T(8,128)(2,1)S(1)}, u32[]{:S(2)}, u32[]{:S(2)}) collective-permute-start(bf16[256,1024]{1,0:T(8,128)(2,1)S(1)} %add_convert_fusion.2), channel_id=1, source_target_pairs={{0,8},{4,12},{8,0},{12,4},{16,24},{20,28},{24,16},{28,20},{1,9},{5... | collective-permute-start | bytes 1572872 | tf_op jit(solution)/shard_map/ppermute | solution.py:15
  85.9 17.4 %collective-permute-start.7 = (bf16[256,1024]{1,0:T(8,128)(2,1)S(1)}, bf16[256,1024]{1,0:T(8,128)(2,1)S(1)}, u32[]{:S(2)}, u32[]{:S(2)}) collective-permute-start(bf16[256,1024]{1,0:T(8,128)(2,1)S(1)} %add_convert_fusion.3), channel_id=1, source_target_pairs={{0,16},{4,20},{8,24},{12,28},{16,0},{20,4},{24,8},{28,12},{1,17},{... | collective-permute-start | bytes 1572872 | tf_op jit(solution)/shard_map/ppermute | solution.py:15
  87.4 30.3 %collective-permute-start.29 = (bf16[256,1024]{1,0:T(8,128)(2,1)S(1)}, bf16[256,1024]{1,0:T(8,128)(2,1)S(1)}, u32[]{:S(2)}, u32[]{:S(2)}) collective-permute-start(bf16[256,1024]{1,0:T(8,128)(2,1)S(1)} %convolution_convert_fusion.6), channel_id=1, source_target_pairs={{0,8},{4,12},{8,0},{12,4},{16,24},{20,28},{24,16},{28,20},{1,9},{5... | collective-permute-start | bytes 1572872 | tf_op jit(solution)/shard_map/ppermute | solution.py:15
  97.1 20.4 %collective-permute-start.34 = (bf16[256,1024]{1,0:T(8,128)(2,1)S(1)}, bf16[256,1024]{1,0:T(8,128)(2,1)S(1)}, u32[]{:S(2)}, u32[]{:S(2)}) collective-permute-start(bf16[256,1024]{1,0:T(8,128)(2,1)S(1)} %add_convert_fusion), channel_id=1, source_target_pairs={{0,8},{4,12},{8,0},{12,4},{16,24},{20,28},{24,16},{28,20},{1,9},{5... | collective-permute-start | bytes 1572872 | tf_op jit(solution)/shard_map/ppermute | solution.py:15
  98.8 19.0 %collective-permute-start.31 = (bf16[256,1024]{1,0:T(8,128)(2,1)S(1)}, bf16[256,1024]{1,0:T(8,128)(2,1)S(1)}, u32[]{:S(2)}, u32[]{:S(2)}) collective-permute-start(bf16[256,1024]{1,0:T(8,128)(2,1)S(1)} %add_convert_fusion.1), channel_id=1, source_target_pairs={{0,16},{4,20},{8,24},{12,28},{16,0},{20,4},{24,8},{28,12},{1,17},{... | collective-permute-start | bytes 1572872 | tf_op jit(solution)/shard_map/ppermute | solution.py:15
  103.5 14.5 %copy-start.3 = (f32[256,1024]{1,0:T(8,128)}, f32[256,1024]{1,0:T(8,128)S(1)}, u32[]{:S(2)}) copy-start(f32[256,1024]{1,0:T(8,128)S(1)} %convert_add_fusion.3) | copy-start | bytes 3145732
  104.7 17.1 %collective-permute-start.25 = (bf16[256,1024]{1,0:T(8,128)(2,1)}, bf16[256,1024]{1,0:T(8,128)(2,1)}, u32[]{:S(2)}, u32[]{:S(2)}) collective-permute-start(bf16[256,1024]{1,0:T(8,128)(2,1)} %fusion.19), channel_id=1, source_target_pairs={{0,1},{1,0},{2,3},{3,2},{4,5},{5,4},{6,7},{7,6},{8,9},{9,8},{10,11... | collective-permute-start | bytes 1572872 | tf_op jit(solution)/shard_map/ppermute | solution.py:79
  117.8 1.5 copy-start.4
  118.0 1.2 copy-start.6
  119.3 31.2 %collective-permute-start.35 = (bf16[256,1024]{1,0:T(8,128)(2,1)}, bf16[256,1024]{1,0:T(8,128)(2,1)}, u32[]{:S(2)}, u32[]{:S(2)}) collective-permute-start(bf16[256,1024]{1,0:T(8,128)(2,1)} %fusion.15), channel_id=1, source_target_pairs={{0,2},{1,3},{2,0},{3,1},{4,6},{5,7},{6,4},{7,5},{8,10},{9,11},{10,... | collective-permute-start | bytes 1572872 | tf_op jit(solution)/shard_map/ppermute | solution.py:79
  121.8 28.7 %copy-start.5 = (f32[256,1024]{1,0:T(8,128)S(1)}, f32[256,1024]{1,0:T(8,128)}, u32[]{:S(2)}) copy-start(f32[256,1024]{1,0:T(8,128)} %copy-done.4) | copy-start | bytes 3145732
  121.8 28.7 %copy-start.7 = (f32[256,1024]{1,0:T(8,128)S(1)}, f32[256,1024]{1,0:T(8,128)}, u32[]{:S(2)}) copy-start(f32[256,1024]{1,0:T(8,128)} %copy-done.6) | copy-start | bytes 3145732
  123.6 31.4 %collective-permute-start.26 = (bf16[128,1024]{1,0:T(8,128)(2,1)S(1)}, bf16[128,1024]{1,0:T(8,128)(2,1)S(1)}, u32[]{:S(2)}, u32[]{:S(2)}) collective-permute-start(bf16[128,1024]{1,0:T(8,128)(2,1)S(1)} %dynamic-slice_convert_fusion.1), channel_id=1, source_target_pairs={{0,2},{1,3},{2,0},{3,1},{4,6},{5,7},{6,4},{7,5},{8,10},{9,11},{10,... | collective-permute-start | bytes 786440 | tf_op jit(solution)/shard_map/ppermute | solution.py:79
  152.5 12.3 %collective-permute-start.36 = (bf16[128,1024]{1,0:T(8,128)(2,1)}, bf16[128,1024]{1,0:T(8,128)(2,1)}, u32[]{:S(2)}, u32[]{:S(2)}) collective-permute-start(bf16[128,1024]{1,0:T(8,128)(2,1)} %dynamic-slice_convert_fusion), channel_id=1, source_target_pairs={{0,1},{1,0},{2,3},{3,2},{4,5},{5,4},{6,7},{7,6},{8,9},{9,8},{10,11... | collective-permute-start | bytes 786440 | tf_op jit(solution)/shard_map/ppermute | solution.py:79
  155.0 10.9 %copy-start.14 = (bf16[128,1024]{1,0:T(8,128)(2,1)}, bf16[128,1024]{1,0:T(8,128)(2,1)S(1)}, u32[]{:S(2)}) copy-start(bf16[128,1024]{1,0:T(8,128)(2,1)S(1)} %add_convert_fusion.5) | copy-start | bytes 786436
  155.1 14.0 %collective-permute-start.27 = (bf16[128,1024]{1,0:T(8,128)(2,1)S(1)}, bf16[128,1024]{1,0:T(8,128)(2,1)}, u32[]{:S(2)}, u32[]{:S(2)}) collective-permute-start(bf16[128,1024]{1,0:T(8,128)(2,1)S(1)} %add_convert_fusion.5), channel_id=1, source_target_pairs={{0,2},{1,3},{2,0},{3,1},{4,6},{5,7},{6,4},{7,5},{8,10},{9,11},{10,... | collective-permute-start | bytes 786440 | tf_op jit(solution)/shard_map/ppermute | solution.py:79
  157.4 26.3 %collective-permute-start.11 = (bf16[256,2048]{1,0:T(8,128)(2,1)}, bf16[256,2048]{1,0:T(8,128)(2,1)}, u32[]{:S(2)}, u32[]{:S(2)}) collective-permute-start(bf16[256,2048]{1,0:T(8,128)(2,1)} %get-tuple-element.22.refs_3_), channel_id=1, source_target_pairs={{0,8},{4,12},{8,0},{12,4},{16,24},{20,28},{24,16},{28,20},{1,9},{5... | collective-permute-start | bytes 3145736 | tf_op jit(solution)/shard_map/ppermute | solution.py:15
  158.8 45.9 %collective-permute-start.19 = (bf16[256,2048]{1,0:T(8,128)(2,1)}, bf16[256,2048]{1,0:T(8,128)(2,1)}, u32[]{:S(2)}, u32[]{:S(2)}) collective-permute-start(bf16[256,2048]{1,0:T(8,128)(2,1)} %get-tuple-element.23.refs_4_), channel_id=1, source_target_pairs={{0,8},{4,12},{8,0},{12,4},{16,24},{20,28},{24,16},{28,20},{1,9},{5... | collective-permute-start | bytes 3145736 | tf_op jit(solution)/shard_map/ppermute | solution.py:15
  165.8 8.8 %collective-permute-start.37 = (bf16[128,1024]{1,0:T(8,128)(2,1)S(1)}, bf16[128,1024]{1,0:T(8,128)(2,1)S(1)}, u32[]{:S(2)}, u32[]{:S(2)}) collective-permute-start(bf16[128,1024]{1,0:T(8,128)(2,1)S(1)} %add_convert_fusion.4), channel_id=1, source_target_pairs={{0,1},{1,0},{2,3},{3,2},{4,5},{5,4},{6,7},{7,6},{8,9},{9,8},{10,11... | collective-permute-start | bytes 786440 | tf_op jit(solution)/shard_map/ppermute | solution.py:79
  170.1 0.7 copy-start.11
  171.7 33.0 %collective-permute-start.28 = (bf16[256,1024]{1,0:T(8,128)(2,1)}, bf16[256,1024]{1,0:T(8,128)(2,1)S(1)}, u32[]{:S(2)}, u32[]{:S(2)}) collective-permute-start(bf16[256,1024]{1,0:T(8,128)(2,1)} %pad_maximum_fusion.5), channel_id=1, source_target_pairs={{0,1},{1,0},{2,3},{3,2},{4,5},{5,4},{6,7},{7,6},{8,9},{9,8},{10,11... | collective-permute-start | bytes 1572872 | tf_op jit(solution)/shard_map/ppermute | solution.py:79
  174.7 1.5 copy-start.13
  176.2 28.9 %collective-permute-start.38 = (bf16[256,1024]{1,0:T(8,128)(2,1)}, bf16[256,1024]{1,0:T(8,128)(2,1)S(1)}, u32[]{:S(2)}, u32[]{:S(2)}) collective-permute-start(bf16[256,1024]{1,0:T(8,128)(2,1)} %pad_maximum_fusion.6), channel_id=1, source_target_pairs={{0,2},{1,3},{2,0},{3,1},{4,6},{5,7},{6,4},{7,5},{8,10},{9,11},{10,... | collective-permute-start | bytes 1572872 | tf_op jit(solution)/shard_map/ppermute | solution.py:79
  178.9 57.1 %copy-start.22 = (f32[512]{0:T(512)}, f32[512]{0:T(512)S(1)}, u32[]{:S(2)}) copy-start(f32[512]{0:T(512)S(1)} %broadcast_divide_fusion.1) | copy-start | bytes 6148
  180.0 52.5 %collective-permute-start.22 = (bf16[256,2048]{1,0:T(8,128)(2,1)}, bf16[256,2048]{1,0:T(8,128)(2,1)}, u32[]{:S(2)}, u32[]{:S(2)}) collective-permute-start(bf16[256,2048]{1,0:T(8,128)(2,1)} %get-tuple-element.22.refs_3_), channel_id=1, source_target_pairs={{0,16},{4,20},{8,24},{12,28},{16,0},{20,4},{24,8},{28,12},{1,17},{... | collective-permute-start | bytes 3145736 | tf_op jit(solution)/shard_map/ppermute | solution.py:15
  183.8 50.1 %collective-permute-start.13 = (bf16[256,2048]{1,0:T(8,128)(2,1)}, bf16[256,2048]{1,0:T(8,128)(2,1)}, u32[]{:S(2)}, u32[]{:S(2)}) collective-permute-start(bf16[256,2048]{1,0:T(8,128)(2,1)} %get-tuple-element.23.refs_4_), channel_id=1, source_target_pairs={{0,16},{4,20},{8,24},{12,28},{16,0},{20,4},{24,8},{28,12},{1,17},{... | collective-permute-start | bytes 3145736 | tf_op jit(solution)/shard_map/ppermute | solution.py:15
  204.6 29.3 %collective-permute-start.17 = (bf16[256,2048]{1,0:T(8,128)(2,1)}, bf16[256,2048]{1,0:T(8,128)(2,1)}, u32[]{:S(2)}, u32[]{:S(2)}) collective-permute-start(bf16[256,2048]{1,0:T(8,128)(2,1)} %get-tuple-element.22.refs_3_), channel_id=1, source_target_pairs={{0,4},{4,0},{8,12},{12,8},{16,20},{20,16},{24,28},{28,24},{1,5},{5... | collective-permute-start | bytes 3145736 | tf_op jit(solution)/shard_map/ppermute | solution.py:15
  204.6 0.8 copy-start.19
  204.6 30.8 %collective-permute-start.18 = (bf16[256,2048]{1,0:T(8,128)(2,1)}, bf16[256,2048]{1,0:T(8,128)(2,1)}, u32[]{:S(2)}, u32[]{:S(2)}) collective-permute-start(bf16[256,2048]{1,0:T(8,128)(2,1)} %get-tuple-element.23.refs_4_), channel_id=1, source_target_pairs={{0,4},{4,0},{8,12},{12,8},{16,20},{20,16},{24,28},{28,24},{1,5},{5... | collective-permute-start | bytes 3145736 | tf_op jit(solution)/shard_map/ppermute | solution.py:15
  205.4 0.8 copy-start.20
  206.2 29.4 %collective-permute-start.20 = (bf16[256,2048]{1,0:T(8,128)(2,1)}, bf16[256,2048]{1,0:T(8,128)(2,1)}, u32[]{:S(2)}, u32[]{:S(2)}) collective-permute-start(bf16[256,2048]{1,0:T(8,128)(2,1)} %collective-permute-done.11.refs_7_), channel_id=1, source_target_pairs={{0,4},{4,0},{8,12},{12,8},{16,20},{20,16},{24,28},{28,24},{1,5},{5... | collective-permute-start | bytes 3145736 | tf_op jit(solution)/shard_map/ppermute | solution.py:15
  209.5 9.6 %copy-start.9 = (bf16[256,1024]{1,0:T(8,128)(2,1)}, bf16[256,1024]{1,0:T(8,128)(2,1)S(1)}, u32[]{:S(2)}) copy-start(bf16[256,1024]{1,0:T(8,128)(2,1)S(1)} %get-tuple-element.46) | copy-start | bytes 1572868
  209.6 9.6 %copy-start.10 = (bf16[256,1024]{1,0:T(8,128)(2,1)}, bf16[256,1024]{1,0:T(8,128)(2,1)S(1)}, u32[]{:S(2)}) copy-start(bf16[256,1024]{1,0:T(8,128)(2,1)S(1)} %get-tuple-element.47) | copy-start | bytes 1572868
  232.6 25.5 %collective-permute-start.12 = (bf16[256,2048]{1,0:T(8,128)(2,1)}, bf16[256,2048]{1,0:T(8,128)(2,1)S(1)}, u32[]{:S(2)}, u32[]{:S(2)}) collective-permute-start(bf16[256,2048]{1,0:T(8,128)(2,1)} %collective-permute-done.11.refs_7_), channel_id=1, source_target_pairs={{0,16},{4,20},{8,24},{12,28},{16,0},{20,4},{24,8},{28,12},{1,17},{... | collective-permute-start | bytes 3145736 | tf_op jit(solution)/shard_map/ppermute | solution.py:15
  233.9 25.8 %collective-permute-start.24 = (bf16[256,2048]{1,0:T(8,128)(2,1)}, bf16[256,2048]{1,0:T(8,128)(2,1)S(1)}, u32[]{:S(2)}, u32[]{:S(2)}) collective-permute-start(bf16[256,2048]{1,0:T(8,128)(2,1)} %collective-permute-done.13.refs_12_), channel_id=1, source_target_pairs={{0,4},{4,0},{8,12},{12,8},{16,20},{20,16},{24,28},{28,24},{1,5},{5... | collective-permute-start | bytes 3145736 | tf_op jit(solution)/shard_map/ppermute | solution.py:15
  233.9 25.8 %collective-permute-start.14 = (bf16[256,2048]{1,0:T(8,128)(2,1)}, bf16[256,2048]{1,0:T(8,128)(2,1)S(1)}, u32[]{:S(2)}, u32[]{:S(2)}) collective-permute-start(bf16[256,2048]{1,0:T(8,128)(2,1)} %collective-permute-done.13.refs_12_), channel_id=1, source_target_pairs={{0,8},{4,12},{8,0},{12,4},{16,24},{20,28},{24,16},{28,20},{1,9},{5... | collective-permute-start | bytes 3145736 | tf_op jit(solution)/shard_map/ppermute | solution.py:15
  235.4 24.3 %collective-permute-start.21 = (bf16[256,2048]{1,0:T(8,128)(2,1)}, bf16[256,2048]{1,0:T(8,128)(2,1)S(1)}, u32[]{:S(2)}, u32[]{:S(2)}) collective-permute-start(bf16[256,2048]{1,0:T(8,128)(2,1)} %collective-permute-done.19.refs_8_), channel_id=1, source_target_pairs={{0,4},{4,0},{8,12},{12,8},{16,20},{20,16},{24,28},{28,24},{1,5},{5... | collective-permute-start | bytes 3145736 | tf_op jit(solution)/shard_map/ppermute | solution.py:15
  235.6 24.1 %collective-permute-start.23 = (bf16[256,2048]{1,0:T(8,128)(2,1)}, bf16[256,2048]{1,0:T(8,128)(2,1)S(1)}, u32[]{:S(2)}, u32[]{:S(2)}) collective-permute-start(bf16[256,2048]{1,0:T(8,128)(2,1)} %collective-permute-done.22.refs_11_), channel_id=1, source_target_pairs={{0,4},{4,0},{8,12},{12,8},{16,20},{20,16},{24,28},{28,24},{1,5},{5... | collective-permute-start | bytes 3145736 | tf_op jit(solution)/shard_map/ppermute | solution.py:15
  258.0 27.0 %copy-start.15 = (bf16[256,2048]{1,0:T(8,128)(2,1)}, bf16[256,2048]{1,0:T(8,128)(2,1)S(1)}, u32[]{:S(2)}) copy-start(bf16[256,2048]{1,0:T(8,128)(2,1)S(1)} %collective-permute-done.12.refs_3_) | copy-start | bytes 3145732
  258.0 27.0 %collective-permute-start.15 = (bf16[256,2048]{1,0:T(8,128)(2,1)S(1)}, bf16[256,2048]{1,0:T(8,128)(2,1)S(1)}, u32[]{:S(2)}, u32[]{:S(2)}) collective-permute-start(bf16[256,2048]{1,0:T(8,128)(2,1)S(1)} %collective-permute-done.12.refs_3_), channel_id=1, source_target_pairs={{0,4},{4,0},{8,12},{12,8},{16,20},{20,16},{24,28},{28,24},{1,5},{5... | collective-permute-start | bytes 3145736 | tf_op jit(solution)/shard_map/ppermute | solution.py:15
  259.7 25.3 %copy-start.16 = (bf16[256,2048]{1,0:T(8,128)(2,1)}, bf16[256,2048]{1,0:T(8,128)(2,1)S(1)}, u32[]{:S(2)}) copy-start(bf16[256,2048]{1,0:T(8,128)(2,1)S(1)} %collective-permute-done.14.refs_4_) | copy-start | bytes 3145732
  259.7 25.3 %collective-permute-start.16 = (bf16[256,2048]{1,0:T(8,128)(2,1)S(1)}, bf16[256,2048]{1,0:T(8,128)(2,1)S(1)}, u32[]{:S(2)}, u32[]{:S(2)}) collective-permute-start(bf16[256,2048]{1,0:T(8,128)(2,1)S(1)} %collective-permute-done.14.refs_4_), channel_id=1, source_target_pairs={{0,4},{4,0},{8,12},{12,8},{16,20},{20,16},{24,28},{28,24},{1,5},{5... | collective-permute-start | bytes 3145736 | tf_op jit(solution)/shard_map/ppermute | solution.py:15
  259.7 1.3 copy-start.24
  259.7 1.0 copy-start.25
  260.7 1.0 copy-start.23
  285.0 1.0 copy-start.17
  285.0 1.3 copy-start.18
  286.4 11.4 %copy-start.1 = (f32[512]{0:T(512)S(1)}, f32[512]{0:T(512)}, u32[]{:S(2)}) copy-start(f32[512]{0:T(512)} %param.7) | copy-start | bytes 6148
  (1 other events, 0.7 us)
